TPU v7x, 32 devices: a whole 2x2x4 slice. The times are simulated.
32 devices in a mesh: row: 4 (over y, x), col: 8 (over z, core).
Axes of the slice: x: 2, y: 2, z: 4, core: 2. Of those that a mesh axis runs over, the one named last changes fastest.
Arguments:
- samples: bfloat16 [8, 4, 256, 16384], P('col', 'row'), may hold values from -6 to 6
- w_start: float32 [32768, 256], P(('row', 'col')), may hold values from 0.005 to 2
- h_start: float32 [256, 2048], P('row', 'col'), may hold values from 0.005 to 2
Outputs:
- w_final: float32 [32768, 256], P(('row', 'col'))
- h_final: float32 [256, 2048], P('row', 'col')
All inputs are finite; a program needn't handle non-finite values.
Results may differ from a plain program's by a relative error of at most 0.0013.
Values may be sent and summed in bfloat16 or wider, within the bound.
A program may use at most 128 MiB of HBM per device.

v0:
```python
import math

import jax
import jax.numpy as jnp
from jax import lax
from jax.sharding import PartitionSpec as P

BINS = 128
ITERS = 2
WIN = 256


def dft_table():
    sample_idx = jnp.arange(WIN, dtype=jnp.int32)
    bin_idx = jnp.arange(BINS, dtype=jnp.int32)
    phases = sample_idx[:, None] * bin_idx[None, :] % WIN
    phases = phases.astype(jnp.float32) * (2.0 * math.pi / WIN)
    shaping = 0.5 - 0.5 * jnp.cos(sample_idx.astype(jnp.float32) * (2.0 * math.pi / WIN))
    shaping = shaping / math.sqrt(3.0 * WIN / 8.0)
    both = jnp.concatenate(
        [shaping[:, None] * jnp.cos(phases), -shaping[:, None] * jnp.sin(phases)], axis=1
    )
    return both.astype(jnp.bfloat16)


def frame_energy(record, table):
    channels = record.shape[0]
    frames = record.reshape(channels, record.shape[1] // WIN, WIN)
    spectrum = jnp.einsum("cfn,nk->fck", frames, table, preferred_element_type=jnp.float32)
    real_part = spectrum[:, :, :BINS]
    imag_part = spectrum[:, :, BINS:]
    energy = (real_part * real_part + imag_part * imag_part).astype(jnp.bfloat16)
    return energy.reshape(energy.shape[0], channels * BINS)


def local_terms(spectra_tile, w_block, h_block):
    recon = jnp.einsum("kf,rk->fr", h_block, w_block, preferred_element_type=jnp.float32)
    quotient = (spectra_tile / recon).astype(jnp.bfloat16)
    h_numer = jnp.einsum("rk,fr->kf", w_block, quotient, preferred_element_type=jnp.float32)
    w_numer = jnp.einsum("fr,kf->rk", quotient, h_block, preferred_element_type=jnp.float32)
    w_colsum = jnp.sum(w_block, axis=0, dtype=jnp.float32)
    h_rowsum = jnp.sum(h_block, axis=1, dtype=jnp.float32)
    return (h_numer, w_numer, w_colsum, h_rowsum)


def local(samples, w_start, h_start):
    table = dft_table()
    record = samples.reshape(samples.shape[2], samples.shape[3])
    energy = frame_energy(record, table)
    spectra_tile = lax.all_to_all(energy, "row", split_axis=1, concat_axis=0, tiled=True)
    w_state = w_start
    h_state = h_start
    for sweep in range(ITERS):
        w_block = lax.all_gather(w_state.astype(jnp.bfloat16), "col", axis=0, tiled=True)
        h_block = lax.all_gather(h_state.astype(jnp.bfloat16), "row", axis=0, tiled=True)
        h_numer, w_numer, w_colsum, h_rowsum = local_terms(spectra_tile, w_block, h_block)
        h_numer, w_colsum = (
            lax.psum_scatter(h_numer, "row", scatter_dimension=0, tiled=True),
            lax.psum_scatter(w_colsum, "row", scatter_dimension=0, tiled=True),
        )
        w_numer = lax.psum_scatter(w_numer, "col", scatter_dimension=0, tiled=True)
        h_rowsum = lax.psum(h_rowsum, "col")
        h_state = h_state * h_numer / w_colsum[:, None]
        w_state = w_state * w_numer / h_rowsum[None, :]
    return (w_state, h_state)


def solution(mesh):
    placed = (P("col", "row", None, None), P(("row", "col"), None), P("row", "col"))
    return jax.shard_map(
        local,
        mesh=mesh,
        in_specs=placed,
        out_specs=(P(("row", "col"), None), P("row", "col")),
        check_vma=False,
    )
```

profile of v0, /device:TPU:0, one launch (start us, length us, event | category | flops | bytes accessed | tf_op | source)
XLA Modules:
  0.0 438.3 jit_solution(7780668172093798984)
XLA Ops:
  7.2 2.1 convert_element_type.68
  9.3 9.4 %copy.27 = bf16[32,8,64,256]{3,2,1,0:T(8,128)(2,1)} copy(bf16[32,8,64,256]{3,1,2,0:T(8,128)(2,1)} %bitcast.32) | data formatting | bytes 16777216
  18.8 0.5 multiply_convert_fusion
  19.3 15.6 %convolution_bitcast_fusion = f32[64,256,256]{1,2,0:T(8,128)} fusion(bf16[256,64,256]{2,1,0:T(8,128)(2,1)} %bitcast.29, bf16[256,128]{0,1:T(8,128)(2,1)S(1)} %get-tuple-element.10, bf16[256,128]{0,1:T(8,128)(2,1)S(1)} %get-tuple-element.11), kind=kOutput, calls=%fused_computation.4 | convolution fusion | flops 2147745792 | bytes 25296896 | tf_op jit(solution)/shard_map/cfn,nk->fck/dot_general | solution.py:29
  34.9 9.0 %fusion.3 = bf16[64,256,128]{1,2,0:T(8,128)(2,1)} fusion(f32[64,256,256]{1,2,0:T(8,128)} %convolution_bitcast_fusion), kind=kLoop, calls=%fused_computation.7 | loop fusion | flops 8388608 | bytes 20971520 | tf_op jit(solution)/shard_map/convert_element_type | solution.py:32
  43.9 6.4 %copy.16 = bf16[64,256,128]{2,1,0:T(8,128)(2,1)} copy(bf16[64,256,128]{1,2,0:T(8,128)(2,1)} %fusion.3) | data formatting | bytes 8388608 | tf_op jit(solution)/shard_map/convert_element_type | solution.py:32
  50.3 7.0 %all_to_all.10 = bf16[64,4,8192]{2,1,0:T(4,128)(2,1)} reshape(bf16[64,256,128]{2,1,0:T(8,128)(2,1)} %copy.16) | data formatting | bytes 8388608 | tf_op jit(solution)/shard_map/all_to_all | solution.py:50
  57.3 6.5 %copy.17 = bf16[64,4,8192]{2,0,1:T(8,128)(2,1)} copy(bf16[64,4,8192]{2,1,0:T(4,128)(2,1)} %all_to_all.10) | data formatting | bytes 8388608 | tf_op jit(solution)/shard_map/all_to_all | solution.py:50
  63.7 5.2 %all-to-all-start = ((bf16[64,4,8192]{2,0,1:T(8,128)(2,1)}), bf16[64,4,8192]{2,0,1:T(8,128)(2,1)}, u32[]{:S(2)}, u32[]{:S(2)}) async-start(bf16[64,4,8192]{2,0,1:T(8,128)(2,1)} %copy.17), calls=%async_computation | async-start | bytes 8388608 | tf_op jit(solution)/shard_map/all_to_all | solution.py:50
  68.9 52.2 %all_gather.12 = bf16[256,256]{1,0:T(8,128)(2,1)S(1)} all-gather(bf16[64,256]{1,0:T(8,128)(2,1)S(1)} %convert_element_type.67), channel_id=1, replica_groups=mesh['row'=4,'col'=8] {'row'}, dimensions={0}, use_global_device_ids=true | all-gather | bytes 163840 | tf_op jit(solution)/shard_map/all_gather | solution.py:55
  121.2 6.4 %convert_element_type.78 = f32[64,4,8192]{2,0,1:T(8,128)} convert(bf16[64,4,8192]{2,0,1:T(8,128)(2,1)} %all-to-all-done) | non-fusion elementwise | flops 2097152 | bytes 12582912 | tf_op jit(solution)/shard_map/convert_element_type | solution.py:38
  127.6 6.5 %fusion.1 = bf16[256,8192]{1,0:T(8,128)(2,1)S(1)} fusion(f32[256,8192]{1,0:T(8,128)} %bitcast.30, bf16[256,256]{1,0:T(8,128)(2,1)S(1)} %all_gather.12, bf16[8192,256]{1,0:T(8,128)(2,1)} %all-gather.3.cloned.1.call-done), kind=kOutput, calls=%fused_computation.3 | convolution fusion | flops 1077936128 | bytes 16908288 | tf_op jit(solution)/shard_map/kf,rk->fr/dot_general | solution.py:37
  134.1 1.9 copy-done.3
  136.0 1.2 convolution_bitcast_fusion.1
  137.3 0.8 copy.23
  138.1 0.0 reduce-scatter.9.cloned.1.call-start
  138.2 6.7 %fusion.17 = f32[8192,256]{1,0:T(8,128)} fusion(bf16[256,8192]{1,0:T(8,128)(2,1)} %copy-done.3, bf16[256,256]{1,0:T(8,128)(2,1)S(1)} %all_gather.12), kind=kOutput, calls=%fused_computation.38 | convolution fusion | flops 1073741824 | bytes 12713984 | tf_op jit(solution)/shard_map/fr,kf->rk/dot_general | solution.py:40
  144.9 0.0 all-gather.5.cloned.1.call-start
  145.0 0.1 copy.18
  145.1 0.5 copy-done.7
  145.6 0.6 dynamic-slice
  146.8 0.1 convert_reduce_fusion.3
  146.9 3.3 convert_reduce_fusion.1
  150.2 8.9 %all-reduce = f32[256]{0:T(256)S(1)} all-reduce(f32[256]{0:T(256)S(1)} %convert_reduce_fusion.1), channel_id=4, replica_groups=mesh['row'=4,'col'=8] {'row'}, use_global_device_ids=true, to_apply=%region_5.6.clone | all-reduce | flops 256 | bytes 2048
  159.1 0.1 dynamic-slice.1
  159.2 4.0 reduce-scatter.13.cloned.1.call-done
  163.2 0.9 copy.24
  164.1 0.1 copy.19
  164.2 8.5 %all_gather.14 = bf16[256,256]{1,0:T(8,128)(2,1)S(1)} all-gather(bf16[64,256]{1,0:T(8,128)(2,1)S(1)} %copy.19), channel_id=1, replica_groups=mesh['row'=4,'col'=8] {'row'}, dimensions={0}, use_global_device_ids=true | all-gather | bytes 163840 | tf_op jit(solution)/shard_map/all_gather | solution.py:55
  172.7 0.1 convert_reduce_fusion.2
  172.8 14.8 %all-reduce.2 = (f32[256]{0:T(256)S(1)}, f32[256]{0:T(256)S(1)}) all-reduce(f32[256]{0:T(256)S(1)} %convert_reduce_fusion.3, f32[256]{0:T(256)S(1)} %convert_reduce_fusion.2), channel_id=1, replica_groups=mesh['row'=4,'col'=8] {'col'}, use_global_device_ids=true, to_apply=%region_2.3 | all-reduce | flops 512 | bytes 4096 | tf_op jit(solution)/shard_map/psum | solution.py:62
  187.6 67.7 %reduce-scatter.9.cloned.1.call-done = f32[1024,256]{1,0:T(8,128)} async-done(((f32[8192,256]{1,0:T(8,128)}), f32[1024,256]{1,0:T(8,128)}) %reduce-scatter.9.cloned.1.call-update) | async-done | bytes 1048592 | tf_op jit(solution)/shard_map/reduce_scatter | solution.py:61
  255.3 2.2 fusion.16
  257.5 0.3 reduce-scatter.15.cloned.1.call-start
  257.8 45.2 %all-gather.5.cloned.1.call-done = bf16[8192,256]{1,0:T(8,128)(2,1)} async-done(((bf16[1024,256]{1,0:T(8,128)(2,1)}), bf16[8192,256]{1,0:T(8,128)(2,1)}) %all-gather.5.cloned.1.call-update) | async-done | bytes 4194320 | tf_op jit(solution)/shard_map/all_gather | solution.py:54
  303.0 6.5 %fusion = bf16[256,8192]{1,0:T(8,128)(2,1)S(1)} fusion(f32[256,8192]{1,0:T(8,128)} %bitcast.31, bf16[256,256]{1,0:T(8,128)(2,1)S(1)} %all_gather.14, bf16[8192,256]{1,0:T(8,128)(2,1)} %all-gather.5.cloned.1.call-done), kind=kOutput, calls=%fused_computation.1 | convolution fusion | flops 1077936128 | bytes 16908288 | tf_op jit(solution)/shard_map/kf,rk->fr/dot_general | solution.py:37
  309.6 1.9 copy-done
  311.5 2.5 fusion.19
  314.1 0.0 reduce-scatter.11.cloned.1.call-start
  314.1 6.7 %fusion.18 = f32[8192,256]{1,0:T(8,128)} fusion(bf16[256,8192]{1,0:T(8,128)(2,1)} %copy-done, bf16[256,256]{1,0:T(8,128)(2,1)S(1)} %all_gather.14), kind=kOutput, calls=%fused_computation.39 | convolution fusion | flops 1073741824 | bytes 12713984 | tf_op jit(solution)/shard_map/fr,kf->rk/dot_general | solution.py:40
  320.9 3.4 convert_reduce_fusion
  324.2 9.9 %all-reduce.1 = f32[256]{0:T(256)S(1)} all-reduce(f32[256]{0:T(256)S(1)} %convert_reduce_fusion), channel_id=7, replica_groups=mesh['row'=4,'col'=8] {'row'}, use_global_device_ids=true, to_apply=%region_11.12.clone | all-reduce | flops 256 | bytes 2048
  334.1 0.1 dynamic-slice.3
  334.2 3.1 reduce-scatter.15.cloned.1.call-done
  337.3 0.9 copy.26
  338.3 0.7 copy.21
  339.0 90.0 %reduce-scatter.11.cloned.1.call-done = f32[1024,256]{1,0:T(8,128)} async-done(((f32[8192,256]{1,0:T(8,128)}), f32[1024,256]{1,0:T(8,128)}) %reduce-scatter.11.cloned.1.call-update) | async-done | bytes 1048592 | tf_op jit(solution)/shard_map/reduce_scatter | solution.py:61
  429.1 2.4 multiply_divide_fusion
  (28 shorter events, 0.3 us)
Async XLA Ops:
  7.2 120.4 %all-gather.3.cloned.1.call-start = ((), (), s32[]{:S(2)}) async-start(), calls=%async_computation.5 | async-start | bytes 4718592 | tf_op jit(solution)/shard_map/all_gather | solution.py:54
  63.7 5.2 %copy-start.6 = (f32[64,256]{1,0:T(8,128)S(1)}, f32[64,256]{1,0:T(8,128)}, u32[]{:S(2)}) copy-start(f32[64,256]{1,0:T(8,128)} %param.5) | copy-start | bytes 196612
  63.7 57.4 %all-to-all-start = ((bf16[64,4,8192]{2,0,1:T(8,128)(2,1)}), bf16[64,4,8192]{2,0,1:T(8,128)(2,1)}, u32[]{:S(2)}, u32[]{:S(2)}) async-start(bf16[64,4,8192]{2,0,1:T(8,128)(2,1)} %copy.17), calls=%async_computation | async-start | bytes 8388608 | tf_op jit(solution)/shard_map/all_to_all | solution.py:50
  68.9 94.3 %reduce-scatter.13.cloned.1.call-start = ((), (), s32[]{:S(2)}) async-start(), calls=%async_computation.9 | async-start | bytes 327680
  127.6 8.5 %copy-start.4 = (bf16[8192,256]{1,0:T(8,128)(2,1)S(1)}, bf16[8192,256]{1,0:T(8,128)(2,1)}, u32[]{:S(2)}) copy-start(bf16[8192,256]{1,0:T(8,128)(2,1)} %all-gather.3.cloned.1.call-done) | copy-start | bytes 12582916
  134.1 1.9 copy-start.3
  138.1 117.2 %reduce-scatter.9.cloned.1.call-start = ((), (), s32[]{:S(2)}) async-start(), calls=%async_computation.6 | async-start | bytes 9437184 | tf_op jit(solution)/shard_map/reduce_scatter | solution.py:61
  144.9 0.7 copy-start.7
  144.9 110.4 %copy-start.2 = (f32[1024,256]{1,0:T(8,128)S(1)}, f32[1024,256]{1,0:T(8,128)}, u32[]{:S(2)}) copy-start(f32[1024,256]{1,0:T(8,128)} %param.4) | copy-start | bytes 3145732
  144.9 158.1 %all-gather.5.cloned.1.call-start = ((), (), s32[]{:S(2)}) async-start(), calls=%async_computation.7 | async-start | bytes 4718592 | tf_op jit(solution)/shard_map/all_gather | solution.py:54
  257.5 79.8 %reduce-scatter.15.cloned.1.call-start = ((), (), s32[]{:S(2)}) async-start(), calls=%async_computation.10 | async-start | bytes 327680
  303.0 8.5 %copy-start.1 = (bf16[8192,256]{1,0:T(8,128)(2,1)S(1)}, bf16[8192,256]{1,0:T(8,128)(2,1)}, u32[]{:S(2)}) copy-start(bf16[8192,256]{1,0:T(8,128)(2,1)} %all-gather.5.cloned.1.call-done) | copy-start | bytes 12582916
  309.5 2.0 copy-start
  314.1 115.0 %reduce-scatter.11.cloned.1.call-start = ((), (), s32[]{:S(2)}) async-start(), calls=%async_computation.8 | async-start | bytes 9437184 | tf_op jit(solution)/shard_map/reduce_scatter | solution.py:61
  320.9 108.2 %copy-start.5 = (f32[1024,256]{1,0:T(8,128)S(1)}, f32[1024,256]{1,0:T(8,128)}, u32[]{:S(2)}) copy-start(f32[1024,256]{1,0:T(8,128)} %reduce-scatter.9.cloned.1.call-done) | copy-start | bytes 3145732
Sparse Core Ops, SparseCore 0:
  10.1 49.5 all-gather.2
  138.3 24.8 reduce-scatter.12
  165.5 89.8 reduce-scatter.8
  257.7 45.3 all-gather.4
  314.2 23.1 reduce-scatter.14
  339.5 89.5 reduce-scatter.10
where the time goes:
time: 439 us; the launch traced here: 438 us
  waiting for transfers between devices  210 us (48%)
  blocking collectives  94.3 us (21%)
  matrix products  45.9 us (10%)
  local copies, waits for them, and re-layouts  37.9 us (9%)
  other arithmetic  29.6 us (7%)
  between operations  14.9 us (3%)
  starting transfers between devices  5.59 us (1%)
    reduce_scatter x2, waiting for transfers between devices, local(): w_numer = lax.psum_scatter(w_numer, 'col', scatter_dimension=0, tiled=True)  158 us
    all_gather x2, blocking collectives, local(): lax.all_gather(h_state.astype(jnp.bfloat16), 'row', axis=0, tiled=True)  60.7 us
    all_gather x2, waiting for transfers between devices, local(): lax.all_gather(w_state.astype(jnp.bfloat16), 'col', axis=0, tiled=True)  45.2 us
    unnamed x2, blocking collectives  18.8 us
    unnamed x25, local copies, waits for them, and re-layouts  18 us
    dot_general x1, matrix products, frame_energy(): jnp.einsum('cfn,nk->fck', frames, table, preferred_element_type=jnp.float32)  15.6 us
    psum x1, blocking collectives, local(): h_rowsum = lax.psum(h_rowsum, 'col')  14.8 us
    dot_general x2, matrix products, local_terms(): jnp.einsum('fr,kf->rk', quotient, h_block, preferred_element_type=jnp.flo...  13.4 us
  transfers between devices with their start and end apart: 7, of which 5 were waited for; matrix products, arithmetic and copies ran while one was open for 18% of the time, Pallas kernels for 0%

commit v1 on v0

v1 whole, which is shorter than its diff:
```python
import functools
import math

import jax
import jax.numpy as jnp
from jax import lax
from jax.experimental import pallas as pl
from jax.experimental.pallas import tpu as pltpu
from jax.sharding import PartitionSpec as P

BINS = 128
ITERS = 2
WIN = 256


def dft_table():
    sample_idx = jnp.arange(WIN, dtype=jnp.int32)
    bin_idx = jnp.arange(BINS, dtype=jnp.int32)
    phases = sample_idx[:, None] * bin_idx[None, :] % WIN
    phases = phases.astype(jnp.float32) * (2.0 * math.pi / WIN)
    shaping = 0.5 - 0.5 * jnp.cos(sample_idx.astype(jnp.float32) * (2.0 * math.pi / WIN))
    shaping = shaping / math.sqrt(3.0 * WIN / 8.0)
    both = jnp.concatenate(
        [shaping[:, None] * jnp.cos(phases), -shaping[:, None] * jnp.sin(phases)], axis=1
    )
    return both.astype(jnp.bfloat16)


MESH = pl.DeviceIdType.MESH


def greet(partners):
    barrier = pltpu.get_barrier_semaphore()
    for row, col in partners:
        pl.semaphore_signal(barrier, inc=1, device_id={"row": row, "col": col}, device_id_type=MESH)
    pl.semaphore_wait(barrier, len(partners))


class Gather:
    def __init__(self, n_row, n_col, out, sends, recvs):
        self.n_row, self.n_col = n_row, n_col
        self.row, self.col = lax.axis_index("row"), lax.axis_index("col")
        self.core, self.chip = lax.rem(self.col, 2), self.col // 2
        self.chips = n_col // 2
        self.out, self.sends, self.recvs = out, sends, recvs

    def chip_partner(self, k):
        return self.row, lax.rem(self.chip + k, self.chips) * 2 + self.core

    def row_partner(self, k):
        return lax.rem(self.row + k, self.n_row), self.col

    def core_partner(self):
        return self.row, self.chip * 2 + 1 - self.core

    def partners(self):
        chips = [self.chip_partner(k) for k in range(1, self.chips)]
        rows = [self.row_partner(k) for k in range(1, self.n_row)]
        return chips + rows + [self.core_partner()]

    def copy(self, src, dst, index, partner):
        return pltpu.make_async_remote_copy(
            src_ref=src,
            dst_ref=dst,
            send_sem=self.sends.at[index],
            recv_sem=self.recvs.at[index],
            device_id={"row": partner[0], "col": partner[1]},
            device_id_type=MESH,
        )

    def chip_copies(self):
        slot = self.out.at[self.row, self.core, self.chip]
        return [self.copy(slot, slot, k - 1, self.chip_partner(k)) for k in range(1, self.chips)]

    def row_copies(self):
        slot = self.out.at[self.row, self.core]
        base = self.chips - 2
        return [self.copy(slot, slot, base + k, self.row_partner(k)) for k in range(1, self.n_row)]

    def core_copies(self):
        base = self.chips + self.n_row - 2
        slots = [self.out.at[r, self.core] for r in range(self.n_row)]
        return [self.copy(s, s, base + r, self.core_partner()) for r, s in enumerate(slots)]

    def place(self, mine):
        self.out[self.row, self.core, self.chip] = mine[...]

    def stage(self, number):
        lists = (self.chip_copies, self.row_copies, self.core_copies)
        if number > 0:
            for copy in lists[number - 1]():
                copy.wait()
        if number < 3:
            for copy in lists[number]():
                copy.start()


def gather_scratch(n_row, n_col, h_b):
    sems = pltpu.SemaphoreType.DMA((n_col // 2 + 2 * n_row,))
    return [pltpu.VMEM((n_row, 2, n_col // 2, *h_b.shape), h_b.dtype), sems, sems]


def gather_kernel(n_row, n_col, h_ref, out_ref, held, sends, recvs):
    gather = Gather(n_row, n_col, held, sends, recvs)
    gather.place(h_ref)
    greet(gather.partners())
    for number in range(4):
        gather.stage(number)
    out_ref[...] = held[...]


def gather_factor(n_row, n_col, h_b):
    return pl.pallas_call(
        functools.partial(gather_kernel, n_row, n_col),
        in_specs=[pl.BlockSpec(memory_space=pltpu.VMEM)],
        out_specs=pl.BlockSpec(memory_space=pltpu.VMEM),
        out_shape=jax.ShapeDtypeStruct((n_row, 2, n_col // 2, *h_b.shape), h_b.dtype),
        scratch_shapes=gather_scratch(n_row, n_col, h_b),
        compiler_params=pltpu.CompilerParams(collective_id=2, has_side_effects=True),
        name="gather_factor",
    )(h_b)


def exchange_kernel(n_row, n_col, x_ref, out_ref, sends, recvs, own_sem):
    n = n_row * n_col
    row, col = lax.axis_index("row"), lax.axis_index("col")
    me = row * n_col + col
    barrier = pltpu.get_barrier_semaphore()

    def partner(k):
        to_row = lax.rem(row + lax.rem(k, n_row), n_row)
        to_col = lax.rem(col + k // n_row, n_col)
        return to_row, to_col

    def signal(k, carry):
        to_row, to_col = partner(k)
        pl.semaphore_signal(
            barrier, inc=1, device_id={"row": to_row, "col": to_col}, device_id_type=MESH
        )
        return carry

    def copy(k):
        to_row, to_col = partner(k)
        return pltpu.make_async_remote_copy(
            src_ref=x_ref.at[to_row * n_col + to_col],
            dst_ref=out_ref.at[me],
            send_sem=sends.at[k],
            recv_sem=recvs.at[k],
            device_id={"row": to_row, "col": to_col},
            device_id_type=MESH,
        )

    def start(k, carry):
        copy(k).start()
        return carry

    def finish(k, carry):
        copy(k).wait()
        return carry

    own = pltpu.make_async_copy(x_ref.at[me], out_ref.at[me], own_sem)
    own.start()
    lax.fori_loop(1, n, signal, 0)
    pl.semaphore_wait(barrier, n - 1)
    lax.fori_loop(1, n, start, 0)
    lax.fori_loop(1, n, finish, 0)
    own.wait()


def exchange(n_row, n_col, x, space, number, name):
    n = n_row * n_col
    return pl.pallas_call(
        functools.partial(exchange_kernel, n_row, n_col),
        in_specs=[pl.BlockSpec(memory_space=space)],
        out_specs=pl.BlockSpec(memory_space=space),
        out_shape=jax.ShapeDtypeStruct(x.shape, x.dtype),
        scratch_shapes=[
            pltpu.SemaphoreType.DMA((n,)),
            pltpu.SemaphoreType.DMA((n,)),
            pltpu.SemaphoreType.DMA,
        ],
        compiler_params=pltpu.CompilerParams(collective_id=number, has_side_effects=True),
        name=name,
    )(x)


def reduce_kernel(
    n_row, n_col, x_ref, out_ref, pair, summed, row_landed, second, chip_landed, sends, recvs
):
    row, col = lax.axis_index("row"), lax.axis_index("col")
    core, chip = lax.rem(col, 2), col // 2
    chips = n_col // 2

    def row_at(k):
        return lax.rem(row + k, n_row)

    def chip_at(k):
        return lax.rem(chip + k, chips)

    mate = (row, chip * 2 + 1 - core)
    greet(
        [mate]
        + [(row_at(k), col) for k in range(1, n_row)]
        + [(row, chip_at(k) * 2 + core) for k in range(1, chips)]
    )

    def copy(src, dst, index, partner):
        return pltpu.make_async_remote_copy(
            src_ref=src,
            dst_ref=dst,
            send_sem=sends.at[index],
            recv_sem=recvs.at[index],
            device_id={"row": partner[0], "col": partner[1]},
            device_id_type=MESH,
        )

    swaps = [copy(x_ref.at[1 - core, row_at(k)], pair.at[k], k, mate) for k in range(n_row)]
    row_copies = [
        copy(summed.at[k], row_landed.at[k], n_row + k, (row_at(k), col)) for k in range(1, n_row)
    ]
    chip_copies = [
        copy(second.at[chip_at(k)], chip_landed.at[k], 2 * n_row + k, (row, chip_at(k) * 2 + core))
        for k in range(1, chips)
    ]
    order = list(range(1, n_row)) + [0]
    for k in order:
        swaps[k].start()
    for k in order:
        swaps[k].wait()
        summed[k] = x_ref[core, row_at(k)] + pair[k]
        if k > 0:
            row_copies[k - 1].start()
    total = summed[0]
    for k in range(1, n_row):
        row_copies[k - 1].wait()
        total = total + row_landed[k]
    second[...] = total
    for c in chip_copies:
        c.start()
    result = second[chip]
    for k in range(1, chips):
        chip_copies[k - 1].wait()
        result = result + chip_landed[k]
    out_ref[...] = result


def reduce_numer(n_row, n_col, x):
    lines, span = x.shape[3:]
    chips = n_col // 2
    return pl.pallas_call(
        functools.partial(reduce_kernel, n_row, n_col),
        in_specs=[pl.BlockSpec(memory_space=pltpu.VMEM)],
        out_specs=pl.BlockSpec(memory_space=pltpu.VMEM),
        out_shape=jax.ShapeDtypeStruct((lines, span), jnp.float32),
        scratch_shapes=[
            pltpu.VMEM((n_row, chips, lines, span), x.dtype),
            pltpu.VMEM((n_row, chips, lines, span), x.dtype),
            pltpu.VMEM((n_row, chips, lines, span), x.dtype),
            pltpu.VMEM((chips, lines, span), x.dtype),
            pltpu.VMEM((chips, lines, span), x.dtype),
            pltpu.SemaphoreType.DMA((2 * n_row + chips,)),
            pltpu.SemaphoreType.DMA((2 * n_row + chips,)),
        ],
        compiler_params=pltpu.CompilerParams(collective_id=4, has_side_effects=True),
        name="reduce_numer",
    )(x)


def energy_kernel(
    frames, group, n_row, n_col, x_ref, table_ref, h_ref, out_ref, h_all_ref, scratch, held, sends, recvs
):
    step = pl.program_id(0)
    gather = Gather(n_row, n_col, held, sends, recvs)

    @pl.when(step == 0)
    def _():
        gather.place(h_ref)
        greet(gather.partners())

    for number in range(4):

        @pl.when(step == 2 * number + 1)
        def _():
            gather.stage(number)

    @pl.when(step == 7)
    def _():
        h_all_ref[...] = held[...]

    channels = x_ref.shape[0]
    table = table_ref[...]
    for first in range(0, frames, group):
        lhs = jnp.concatenate(
            [x_ref[:, f * WIN : (f + 1) * WIN] for f in range(first, first + group)], axis=0
        )
        spectrum = jnp.dot(lhs, table, preferred_element_type=jnp.float32)
        real_part = spectrum[:, :BINS]
        imag_part = spectrum[:, BINS:]
        scratch[pl.ds(first * channels, group * channels), :] = (
            real_part * real_part + imag_part * imag_part
        )
    for ch in range(channels):
        out_ref[ch] = scratch[pl.ds(ch, frames, stride=channels), :].astype(jnp.bfloat16)


def frame_energy(n_row, n_col, record, table, h_b):
    channels, samples = record.shape
    frames = samples // WIN
    block = 32
    assert channels // block >= 8
    return pl.pallas_call(
        functools.partial(energy_kernel, frames, 16, n_row, n_col),
        grid=(channels // block,),
        in_specs=[
            pl.BlockSpec((block, samples), lambda i: (i, 0)),
            pl.BlockSpec((WIN, 2 * BINS), lambda i: (0, 0)),
            pl.BlockSpec(memory_space=pltpu.VMEM),
        ],
        out_specs=[
            pl.BlockSpec((block, frames, BINS), lambda i: (i, 0, 0)),
            pl.BlockSpec(memory_space=pltpu.VMEM),
        ],
        out_shape=[
            jax.ShapeDtypeStruct((channels, frames, BINS), jnp.bfloat16),
            jax.ShapeDtypeStruct((n_row, 2, n_col // 2, *h_b.shape), h_b.dtype),
        ],
        scratch_shapes=[pltpu.VMEM((frames * block, BINS), jnp.float32)]
        + gather_scratch(n_row, n_col, h_b),
        compiler_params=pltpu.CompilerParams(collective_id=1, has_side_effects=True),
        name="frame_energy",
    )(record, table, h_b)


def sweep_kernel(spectra_ref, w_ref, h_ref, numer_ref, w_out_ref, w_b, wt_b, wn_t, rowsum, colsum):
    step = pl.program_id(0)
    n_row, _, chans, frames, bins = spectra_ref.shape
    ranks = h_ref.shape[3]

    @pl.when(step == 0)
    def _():
        w_b[...] = w_ref[...].astype(jnp.bfloat16)
        wt_b[...] = w_ref[...].T.astype(jnp.bfloat16)
        wn_t[...] = jnp.zeros_like(wn_t)
        colsum[...] = jnp.zeros_like(colsum)
        rowsum[...] = jnp.zeros_like(rowsum)
        total = jnp.sum(w_b[...].astype(jnp.float32), axis=0, keepdims=True)
        line = lax.broadcasted_iota(jnp.int32, (colsum.shape[0], total.shape[1]), 0)
        colsum[:, : total.shape[1]] = jnp.where(line == 0, total, 0.0)

    h_b = jnp.concatenate([h_ref[r, 0, 0] for r in range(n_row)], axis=0)
    h_f = h_b.astype(jnp.float32)
    rowsum[...] += jnp.sum(h_f, axis=1, keepdims=True)
    ht_b = h_f.T.astype(jnp.bfloat16)
    recon = jnp.dot(ht_b, wt_b[...], preferred_element_type=jnp.float32)
    tile = jnp.concatenate(
        [
            jnp.concatenate([spectra_ref[r, 0, c] for c in range(chans)], axis=1)
            for r in range(n_row)
        ],
        axis=0,
    )
    quotient = (tile.astype(jnp.float32) / recon).astype(jnp.bfloat16)
    hn = jnp.dot(quotient, w_b[...], preferred_element_type=jnp.float32).T
    wn_t[...] += jnp.dot(h_b, quotient, preferred_element_type=jnp.float32)
    for r in range(n_row):
        numer_ref[0, r, 0, :ranks, :] = hn[r * ranks : (r + 1) * ranks]
        numer_ref[0, r, 0, ranks:, :] = colsum[...]

    @pl.when(step == pl.num_programs(0) - 1)
    def _():
        w_out_ref[...] = w_ref[...] * (wn_t[...] / rowsum[...]).T


def sweep_terms(spectra, w_state, h_all):
    n_row, n_col, chans, frames, bins = spectra.shape
    rows, rank = w_state.shape
    ranks, span = h_all.shape[3:]
    lines = ranks + 8
    assert span >= rank
    return pl.pallas_call(
        sweep_kernel,
        grid=(n_col,),
        in_specs=[
            pl.BlockSpec((n_row, 1, chans, frames, bins), lambda i: (0, i, 0, 0, 0)),
            pl.BlockSpec((rows, rank), lambda i: (0, 0)),
            pl.BlockSpec((n_row, 1, 1, ranks, span), lambda i: (0, i % 2, i // 2, 0, 0)),
        ],
        out_specs=[
            pl.BlockSpec((1, n_row, 1, lines, span), lambda i: (i % 2, 0, i // 2, 0, 0)),
            pl.BlockSpec((rows, rank), lambda i: (0, 0)),
        ],
        out_shape=[
            jax.ShapeDtypeStruct((2, n_row, n_col // 2, lines, span), jnp.float32),
            jax.ShapeDtypeStruct((rows, rank), jnp.float32),
        ],
        scratch_shapes=[
            pltpu.VMEM((rows, rank), jnp.bfloat16),
            pltpu.VMEM((rank, rows), jnp.bfloat16),
            pltpu.VMEM((rank, rows), jnp.float32),
            pltpu.VMEM((rank, 1), jnp.float32),
            pltpu.VMEM((8, span), jnp.float32),
        ],
        name="sweep_terms",
    )(spectra, w_state, h_all)


def local(n_row, n_col, samples, w_start, h_start):
    n = n_row * n_col
    table = dft_table()
    record = samples.reshape(samples.shape[2], samples.shape[3])
    energy, h_all = frame_energy(n_row, n_col, record, table, h_start.astype(jnp.bfloat16))
    channels, frames, bins = energy.shape
    energy = energy.reshape(n, channels // n, frames, bins)
    spectra = exchange(n_row, n_col, energy, pl.ANY, 3, "exchange_spectra")
    spectra = spectra.reshape(n_row, n_col, channels // n, frames, bins)
    ranks, span = h_start.shape
    rank = w_start.shape[1]
    w_state = w_start
    h_state = h_start
    first = lax.axis_index("row") * ranks
    for sweep in range(ITERS):
        if sweep > 0:
            h_all = gather_factor(n_row, n_col, h_state.astype(jnp.bfloat16))
        numer, w_state = sweep_terms(spectra, w_state, h_all)
        total = reduce_numer(n_row, n_col, numer)
        colsum = total[ranks, :rank]
        colsum = lax.dynamic_slice(colsum, (first,), (ranks,))
        h_state = h_state * total[:ranks] / colsum[:, None]
    return (w_state, h_state)


def solution(mesh):
    placed = (P("col", "row", None, None), P(("row", "col"), None), P("row", "col"))
    return jax.shard_map(
        functools.partial(local, mesh.shape["row"], mesh.shape["col"]),
        mesh=mesh,
        in_specs=placed,
        out_specs=(P(("row", "col"), None), P("row", "col")),
        check_vma=False,
    )
```

time: 439 us -> 224 us (0.51)
  Pallas kernels: 0 us -> 215 us
  waiting for transfers between devices: 210 us -> 0 us
  blocking collectives: 94.3 us -> 0 us
  matrix products: 45.9 us -> 0 us
  local copies, waits for them, and re-layouts: 37.9 us -> 1.55 us
  other arithmetic: 29.6 us -> 5.87 us
  between operations: 14.9 us -> 0.7 us
  starting transfers between devices: 5.59 us -> 0 us
    pallas_call x0 -> x7, Pallas kernels: none -> 215 us  [the longest x2 79.1 us: reduce_numer(): pl.pallas_call(functools.partial(reduce_kernel, n_row, n_col), in_specs=[...]
    reduce_scatter x2 -> x0, waiting for transfers between devices: 158 us -> none  [local(): w_numer = lax.psum_scatter(w_numer, 'col', scatter_dimension=0, tiled=True)]
    all_gather x2 -> x0, blocking collectives: 60.7 us -> none  [local(): lax.all_gather(h_state.astype(jnp.bfloat16), 'row', axis=0, tiled=True)]
    all_gather x2 -> x0, waiting for transfers between devices: 45.2 us -> none  [local(): lax.all_gather(w_state.astype(jnp.bfloat16), 'col', axis=0, tiled=True)]
    dot_general x6 -> x0, matrix products: 43.3 us -> none  [the longest x1 15.6 us: frame_energy(): jnp.einsum('cfn,nk->fck', frames, table, preferred_element_type=jnp.float32)]
    unnamed x2 -> x0, blocking collectives: 18.8 us -> none
    unnamed x25 -> x4, local copies, waits for them, and re-layouts: 18 us -> 0.01 us
    convert_element_type x6 -> x2, other arithmetic: 19.6 us -> 3 us  [the longest x1 1.54 us: local(): h_all = gather_factor(n_row, n_col, h_state.astype(jnp.bfloat16))]
  transfers between devices with their start and end apart: 7 -> 0, of which waited for: 5 -> 0; matrix products, arithmetic and copies ran while one was open for 18% -> 0% of each run, Pallas kernels for 0% -> 0%
where the time goes in v1:
time: 224 us; the launch traced here: 223 us
  Pallas kernels  215 us (96%)
  other arithmetic  5.87 us (3%)
    pallas_call x2, Pallas kernels, reduce_numer(): pl.pallas_call(functools.partial(reduce_kernel, n_row, n_col), in_specs=[...  79.1 us
    pallas_call x1, Pallas kernels, exchange(): pl.pallas_call(functools.partial(exchange_kernel, n_row, n_col), in_specs...  75.3 us
    pallas_call x1, Pallas kernels, frame_energy(): pl.pallas_call(functools.partial(energy_kernel, frames, 16, n_row, n_col)...  22.8 us
    pallas_call x2, Pallas kernels, sweep_terms(): pl.pallas_call(sweep_kernel, grid=(n_col,), in_specs=[pl.BlockSpec((n_row...  21.1 us
    pallas_call x1, Pallas kernels, gather_factor(): pl.pallas_call(functools.partial(gather_kernel, n_row, n_col), in_specs=[...  16.7 us

profile of v1, /device:TPU:0, one launch (start us, length us, event | category | flops | bytes accessed | tf_op | source)
XLA Modules:
  0.0 223.2 jit_solution(16827662097318461479)
XLA Ops:
  0.7 1.5 convert_element_type.26.h_ref
  2.2 0.5 multiply_convert_fusion
  2.7 0.7 pad_maximum_fusion.table_ref
  3.4 22.8 %frame_energy.1 = (bf16[256,64,128]{2,1,0:T(8,128)(2,1)}, bf16[4,2,4,64,256]{4,3,2,1,0:T(8,128)(2,1)}) custom-call(bf16[256,16384]{1,0:T(8,128)(2,1)} %bitcast.9, bf16[256,256]{1,0:T(8,128)(2,1)} %pad_maximum_fusion.table_ref, bf16[64,256]{1,0:T(8,128)(2,1)} %convert_element_type.26.h_ref), custom_call_target="tpu_custom_call" | custom-call | tf_op jit(solution)/shard_map/frame_energy/pallas_call | solution.py:311
  26.2 75.3 %exchange_spectra.1 = bf16[32,8,64,128]{3,2,1,0:T(8,128)(2,1)} custom-call(bf16[32,8,64,128]{3,2,1,0:T(8,128)(2,1)} %bitcast.10), custom_call_target="tpu_custom_call" | custom-call | tf_op jit(solution)/shard_map/exchange_spectra/pallas_call | solution.py:172
  101.6 0.0 copy-start
  101.6 10.6 %sweep_terms.2 = (f32[2,4,4,72,256]{4,3,2,1,0:T(8,128)}, f32[1024,256]{1,0:T(8,128)}) custom-call(bf16[4,8,8,64,128]{4,3,2,1,0:T(8,128)(2,1)} %bitcast.7, f32[1024,256]{1,0:T(8,128)} %w_ref.1, bf16[4,2,4,64,256]{4,3,2,1,0:T(8,128)(2,1)} %get-tuple-element.9.h_ref), custom_call_target="tpu_custom_call" | custom-call | tf_op jit(solution)/shard_map/sweep_terms/pallas_call | solution.py:380
  112.2 50.9 %reduce_numer.2 = f32[72,256]{1,0:T(8,128)} custom-call(f32[2,4,4,72,256]{4,3,2,1,0:T(8,128)} %get-tuple-element.11.x_ref), custom_call_target="tpu_custom_call" | custom-call | tf_op jit(solution)/shard_map/reduce_numer/pallas_call | solution.py:250
  163.0 0.7 slice.13
  163.7 0.1 dynamic-slice_bitcast_fusion.1
  163.8 0.0 copy-done
  163.8 1.5 fusion.7.h_ref
  165.4 16.7 %gather_factor.1.h_ref = bf16[4,2,4,64,256]{4,3,2,1,0:T(8,128)(2,1)} custom-call(bf16[64,256]{1,0:T(8,128)(2,1)} %fusion.7.h_ref), custom_call_target="tpu_custom_call" | custom-call | tf_op jit(solution)/shard_map/gather_factor/pallas_call | solution.py:113
  182.0 0.0 copy-start.1
  182.0 10.6 %sweep_terms.3 = (f32[2,4,4,72,256]{4,3,2,1,0:T(8,128)}, f32[1024,256]{1,0:T(8,128)}) custom-call(bf16[4,8,8,64,128]{4,3,2,1,0:T(8,128)(2,1)} %bitcast.8, f32[1024,256]{1,0:T(8,128)} %get-tuple-element.10.w_ref, bf16[4,2,4,64,256]{4,3,2,1,0:T(8,128)(2,1)} %gather_factor.1.h_ref), custom_call_target="tpu_custom_call" | custom-call | tf_op jit(solution)/shard_map/sweep_terms/pallas_call | solution.py:380
  192.6 28.2 %reduce_numer.3 = f32[72,256]{1,0:T(8,128)} custom-call(f32[2,4,4,72,256]{4,3,2,1,0:T(8,128)} %get-tuple-element.13.x_ref), custom_call_target="tpu_custom_call" | custom-call | tf_op jit(solution)/shard_map/reduce_numer/pallas_call | solution.py:250
  220.8 0.7 slice.15
  221.5 0.1 dynamic-slice_bitcast_fusion
  221.6 0.0 copy-done.1
  221.6 1.6 multiply_divide_fusion
  (2 shorter events, 0.1 us)
Async XLA Ops:
  101.6 62.2 %copy-start = (f32[64,256]{1,0:T(8,128)S(1)}, f32[64,256]{1,0:T(8,128)}, u32[]{:S(2)}) copy-start(f32[64,256]{1,0:T(8,128)} %param.5) | copy-start | bytes 196612
  182.0 39.6 %copy-start.1 = (f32[72,256]{1,0:T(8,128)S(1)}, f32[72,256]{1,0:T(8,128)}, u32[]{:S(2)}) copy-start(f32[72,256]{1,0:T(8,128)} %reduce_numer.2) | copy-start | bytes 221188

commit v2 on v1

--- a/solution.py
+++ b/solution.py
@@ -119,69 +119,6 @@
         compiler_params=pltpu.CompilerParams(collective_id=2, has_side_effects=True),
         name="gather_factor",
     )(h_b)
-
-
-def exchange_kernel(n_row, n_col, x_ref, out_ref, sends, recvs, own_sem):
-    n = n_row * n_col
-    row, col = lax.axis_index("row"), lax.axis_index("col")
-    me = row * n_col + col
-    barrier = pltpu.get_barrier_semaphore()
-
-    def partner(k):
-        to_row = lax.rem(row + lax.rem(k, n_row), n_row)
-        to_col = lax.rem(col + k // n_row, n_col)
-        return to_row, to_col
-
-    def signal(k, carry):
-        to_row, to_col = partner(k)
-        pl.semaphore_signal(
-            barrier, inc=1, device_id={"row": to_row, "col": to_col}, device_id_type=MESH
-        )
-        return carry
-
-    def copy(k):
-        to_row, to_col = partner(k)
-        return pltpu.make_async_remote_copy(
-            src_ref=x_ref.at[to_row * n_col + to_col],
-            dst_ref=out_ref.at[me],
-            send_sem=sends.at[k],
-            recv_sem=recvs.at[k],
-            device_id={"row": to_row, "col": to_col},
-            device_id_type=MESH,
-        )
-
-    def start(k, carry):
-        copy(k).start()
-        return carry
-
-    def finish(k, carry):
-        copy(k).wait()
-        return carry
-
-    own = pltpu.make_async_copy(x_ref.at[me], out_ref.at[me], own_sem)
-    own.start()
-    lax.fori_loop(1, n, signal, 0)
-    pl.semaphore_wait(barrier, n - 1)
-    lax.fori_loop(1, n, start, 0)
-    lax.fori_loop(1, n, finish, 0)
-    own.wait()
-
-
-def exchange(n_row, n_col, x, space, number, name):
-    n = n_row * n_col
-    return pl.pallas_call(
-        functools.partial(exchange_kernel, n_row, n_col),
-        in_specs=[pl.BlockSpec(memory_space=space)],
-        out_specs=pl.BlockSpec(memory_space=space),
-        out_shape=jax.ShapeDtypeStruct(x.shape, x.dtype),
-        scratch_shapes=[
-            pltpu.SemaphoreType.DMA((n,)),
-            pltpu.SemaphoreType.DMA((n,)),
-            pltpu.SemaphoreType.DMA,
-        ],
-        compiler_params=pltpu.CompilerParams(collective_id=number, has_side_effects=True),
-        name=name,
-    )(x)
 
 
 def reduce_kernel(
@@ -266,28 +203,105 @@
     )(x)
 
 
+def first_block(n_row, n_col, blocks):
+    me = lax.axis_index("row") * n_col + lax.axis_index("col")
+    return me * blocks // (n_row * n_col)
+
+
 def energy_kernel(
-    frames, group, n_row, n_col, x_ref, table_ref, h_ref, out_ref, h_all_ref, scratch, held, sends, recvs
+    frames,
+    group,
+    n_row,
+    n_col,
+    x_ref,
+    table_ref,
+    h_ref,
+    out_ref,
+    h_all_ref,
+    scratch,
+    energy,
+    block_sends,
+    block_recvs,
+    own_sem,
+    held,
+    sends,
+    recvs,
 ):
-    step = pl.program_id(0)
+    step, steps = pl.program_id(0), pl.num_programs(0)
     gather = Gather(n_row, n_col, held, sends, recvs)
+    n = n_row * n_col
+    row, col = lax.axis_index("row"), lax.axis_index("col")
+    me = row * n_col + col
+    channels = x_ref.shape[0]
+    chans = out_ref.shape[1]
+    per = channels // chans
+    start_block = first_block(n_row, n_col, n // per)
+
+    def block_copy(target):
+        shift = lax.rem(target - me + n, n)
+        return pltpu.make_async_remote_copy(
+            src_ref=energy.at[pl.ds(target * chans, chans)],
+            dst_ref=out_ref.at[me],
+            send_sem=block_sends.at[shift],
+            recv_sem=block_recvs.at[shift],
+            device_id={"row": target // n_col, "col": lax.rem(target, n_col)},
+            device_id_type=MESH,
+        )
+
+    def own_copy():
+        return pltpu.make_async_copy(
+            energy.at[pl.ds(me * chans, chans)], out_ref.at[me], own_sem
+        )
+
+    def send_block(number):
+        base = lax.rem(start_block + number, n // per) * per
+
+        def send(j, carry):
+            target = base + lax.rem(j + me, per)
+
+            @pl.when(target != me)
+            def _():
+                block_copy(target).start()
+
+            @pl.when(target == me)
+            def _():
+                own_copy().start()
+
+            return carry
+
+        lax.fori_loop(0, per, send, 0)
 
     @pl.when(step == 0)
     def _():
+        barrier = pltpu.get_barrier_semaphore()
         gather.place(h_ref)
-        greet(gather.partners())
-
-    for number in range(4):
-
-        @pl.when(step == 2 * number + 1)
-        def _():
-            gather.stage(number)
-
-    @pl.when(step == 7)
-    def _():
-        h_all_ref[...] = held[...]
-
-    channels = x_ref.shape[0]
+
+        def signal(k, carry):
+            target = lax.rem(me + k, n)
+            pl.semaphore_signal(
+                barrier,
+                inc=1,
+                device_id={"row": target // n_col, "col": lax.rem(target, n_col)},
+                device_id_type=MESH,
+            )
+            return carry
+
+        lax.fori_loop(1, n, signal, 0)
+        pl.semaphore_wait(barrier, n - 1)
+        gather.stage(0)
+
+    @pl.when(step == 1)
+    def _():
+        gather.stage(1)
+
+    @pl.when(step == 4)
+    def _():
+        gather.stage(2)
+
+    @pl.when(step >= 1)
+    def _():
+        send_block(step - 1)
+
     table = table_ref[...]
     for first in range(0, frames, group):
         lhs = jnp.concatenate(
@@ -299,32 +313,59 @@
         scratch[pl.ds(first * channels, group * channels), :] = (
             real_part * real_part + imag_part * imag_part
         )
+    base_channel = lax.rem(start_block + step, n // per) * channels
     for ch in range(channels):
-        out_ref[ch] = scratch[pl.ds(ch, frames, stride=channels), :].astype(jnp.bfloat16)
+        energy[base_channel + ch] = scratch[pl.ds(ch, frames, stride=channels), :].astype(
+            jnp.bfloat16
+        )
+
+    @pl.when(step == steps - 1)
+    def _():
+        send_block(step)
+        gather.stage(3)
+        h_all_ref[...] = held[...]
+
+        def finish(k, carry):
+            block_copy(lax.rem(me + k, n)).wait()
+            return carry
+
+        lax.fori_loop(1, n, finish, 0)
+        own_copy().wait()
 
 
 def frame_energy(n_row, n_col, record, table, h_b):
     channels, samples = record.shape
     frames = samples // WIN
     block = 32
-    assert channels // block >= 8
+    n = n_row * n_col
+    blocks = channels // block
+    assert blocks >= 6 and n % blocks == 0
     return pl.pallas_call(
         functools.partial(energy_kernel, frames, 16, n_row, n_col),
-        grid=(channels // block,),
+        grid=(blocks,),
         in_specs=[
-            pl.BlockSpec((block, samples), lambda i: (i, 0)),
+            pl.BlockSpec(
+                (block, samples),
+                lambda i: (lax.rem(first_block(n_row, n_col, blocks) + i, blocks), 0),
+            ),
             pl.BlockSpec((WIN, 2 * BINS), lambda i: (0, 0)),
             pl.BlockSpec(memory_space=pltpu.VMEM),
         ],
         out_specs=[
-            pl.BlockSpec((block, frames, BINS), lambda i: (i, 0, 0)),
+            pl.BlockSpec(memory_space=pl.ANY),
             pl.BlockSpec(memory_space=pltpu.VMEM),
         ],
         out_shape=[
-            jax.ShapeDtypeStruct((channels, frames, BINS), jnp.bfloat16),
+            jax.ShapeDtypeStruct((n, channels // n, frames, BINS), jnp.bfloat16),
             jax.ShapeDtypeStruct((n_row, 2, n_col // 2, *h_b.shape), h_b.dtype),
         ],
-        scratch_shapes=[pltpu.VMEM((frames * block, BINS), jnp.float32)]
+        scratch_shapes=[
+            pltpu.VMEM((frames * block, BINS), jnp.float32),
+            pltpu.VMEM((channels, frames, BINS), jnp.bfloat16),
+            pltpu.SemaphoreType.DMA((n,)),
+            pltpu.SemaphoreType.DMA((n,)),
+            pltpu.SemaphoreType.DMA,
+        ]
         + gather_scratch(n_row, n_col, h_b),
         compiler_params=pltpu.CompilerParams(collective_id=1, has_side_effects=True),
         name="frame_energy",
@@ -405,14 +446,11 @@
 
 
 def local(n_row, n_col, samples, w_start, h_start):
-    n = n_row * n_col
     table = dft_table()
     record = samples.reshape(samples.shape[2], samples.shape[3])
-    energy, h_all = frame_energy(n_row, n_col, record, table, h_start.astype(jnp.bfloat16))
-    channels, frames, bins = energy.shape
-    energy = energy.reshape(n, channels // n, frames, bins)
-    spectra = exchange(n_row, n_col, energy, pl.ANY, 3, "exchange_spectra")
-    spectra = spectra.reshape(n_row, n_col, channels // n, frames, bins)
+    spectra, h_all = frame_energy(n_row, n_col, record, table, h_start.astype(jnp.bfloat16))
+    n, chans, frames, bins = spectra.shape
+    spectra = spectra.reshape(n_row, n_col, chans, frames, bins)
     ranks, span = h_start.shape
     rank = w_start.shape[1]
     w_state = w_start

time: 224 us -> 211 us (0.942)
  Pallas kernels: 215 us -> 202 us
    pallas_call x1, Pallas kernels: 22.8 us -> 105 us  [frame_energy(): pl.pallas_call(functools.partial(energy_kernel, frames, 16, n_row, n_col)...]
    pallas_call x1 -> x0, Pallas kernels: 75.3 us -> none  [exchange(): pl.pallas_call(functools.partial(exchange_kernel, n_row, n_col), in_specs...]
    pallas_call x2, Pallas kernels: 79.1 us -> 59.9 us  [reduce_numer(): pl.pallas_call(functools.partial(reduce_kernel, n_row, n_col), in_specs=[...]
where the time goes in v2:
time: 211 us; the launch traced here: 210 us
  Pallas kernels  202 us (96%)
  other arithmetic  5.87 us (3%)
    pallas_call x1, Pallas kernels, frame_energy(): pl.pallas_call(functools.partial(energy_kernel, frames, 16, n_row, n_col)...  105 us
    pallas_call x2, Pallas kernels, reduce_numer(): pl.pallas_call(functools.partial(reduce_kernel, n_row, n_col), in_specs=[...  59.9 us
    pallas_call x2, Pallas kernels, sweep_terms(): pl.pallas_call(sweep_kernel, grid=(n_col,), in_specs=[pl.BlockSpec((n_row...  21.1 us
    pallas_call x1, Pallas kernels, gather_factor(): pl.pallas_call(functools.partial(gather_kernel, n_row, n_col), in_specs=[...  16.1 us

profile of v2, /device:TPU:0, one launch (start us, length us, event | category | flops | bytes accessed | tf_op | source)
XLA Modules:
  0.0 210.4 jit_solution(2673057651910338522)
XLA Ops:
  0.7 1.5 convert_element_type.26.h_ref
  2.2 0.5 multiply_convert_fusion
  2.7 0.7 pad_maximum_fusion.table_ref
  3.4 105.1 %frame_energy.1 = (bf16[32,8,64,128]{3,2,1,0:T(8,128)(2,1)}, bf16[4,2,4,64,256]{4,3,2,1,0:T(8,128)(2,1)}) custom-call(bf16[256,16384]{1,0:T(8,128)(2,1)} %bitcast.8, bf16[256,256]{1,0:T(8,128)(2,1)} %pad_maximum_fusion.table_ref, bf16[64,256]{1,0:T(8,128)(2,1)} %convert_element_type.26.h_ref), custom_call_target="tpu_custom_call" | custom-call | tf_op jit(solution)/shard_map/frame_energy/pallas_call | solution.py:343
  108.5 0.0 copy-start
  108.5 10.6 %sweep_terms.2 = (f32[2,4,4,72,256]{4,3,2,1,0:T(8,128)}, f32[1024,256]{1,0:T(8,128)}) custom-call(bf16[4,8,8,64,128]{4,3,2,1,0:T(8,128)(2,1)} %bitcast.6, f32[1024,256]{1,0:T(8,128)} %w_ref.1, bf16[4,2,4,64,256]{4,3,2,1,0:T(8,128)(2,1)} %get-tuple-element.9.h_ref), custom_call_target="tpu_custom_call" | custom-call | tf_op jit(solution)/shard_map/sweep_terms/pallas_call | solution.py:421
  119.1 31.4 %reduce_numer.2 = f32[72,256]{1,0:T(8,128)} custom-call(f32[2,4,4,72,256]{4,3,2,1,0:T(8,128)} %get-tuple-element.11.x_ref), custom_call_target="tpu_custom_call" | custom-call | tf_op jit(solution)/shard_map/reduce_numer/pallas_call | solution.py:187
  150.4 0.7 slice.13
  151.1 0.1 dynamic-slice_bitcast_fusion.1
  151.2 0.0 copy-done
  151.2 1.5 fusion.7.h_ref
  152.8 16.1 %gather_factor.1.h_ref = bf16[4,2,4,64,256]{4,3,2,1,0:T(8,128)(2,1)} custom-call(bf16[64,256]{1,0:T(8,128)(2,1)} %fusion.7.h_ref), custom_call_target="tpu_custom_call" | custom-call | tf_op jit(solution)/shard_map/gather_factor/pallas_call | solution.py:113
  168.9 0.0 copy-start.1
  168.9 10.6 %sweep_terms.3 = (f32[2,4,4,72,256]{4,3,2,1,0:T(8,128)}, f32[1024,256]{1,0:T(8,128)}) custom-call(bf16[4,8,8,64,128]{4,3,2,1,0:T(8,128)(2,1)} %bitcast.7, f32[1024,256]{1,0:T(8,128)} %get-tuple-element.10.w_ref, bf16[4,2,4,64,256]{4,3,2,1,0:T(8,128)(2,1)} %gather_factor.1.h_ref), custom_call_target="tpu_custom_call" | custom-call | tf_op jit(solution)/shard_map/sweep_terms/pallas_call | solution.py:421
  179.5 28.6 %reduce_numer.3 = f32[72,256]{1,0:T(8,128)} custom-call(f32[2,4,4,72,256]{4,3,2,1,0:T(8,128)} %get-tuple-element.13.x_ref), custom_call_target="tpu_custom_call" | custom-call | tf_op jit(solution)/shard_map/reduce_numer/pallas_call | solution.py:187
  208.0 0.7 slice.15
  208.7 0.1 dynamic-slice_bitcast_fusion
  208.8 0.0 copy-done.1
  208.8 1.6 multiply_divide_fusion
  (2 shorter events, 0.1 us)
Async XLA Ops:
  108.5 42.7 %copy-start = (f32[64,256]{1,0:T(8,128)S(1)}, f32[64,256]{1,0:T(8,128)}, u32[]{:S(2)}) copy-start(f32[64,256]{1,0:T(8,128)} %param.5) | copy-start | bytes 196612
  168.9 39.9 %copy-start.1 = (f32[72,256]{1,0:T(8,128)S(1)}, f32[72,256]{1,0:T(8,128)}, u32[]{:S(2)}) copy-start(f32[72,256]{1,0:T(8,128)} %reduce_numer.2) | copy-start | bytes 221188
